TPU v7x, 32 devices: a whole 2x2x4 slice. The times are simulated.
32 devices in a mesh: dp: 8 (over z, y), head: 4 (over x, core).
Axes of the slice: x: 2, y: 2, z: 4, core: 2. Of those that a mesh axis runs over, the one named last changes fastest.
Arguments:
- tokens: bfloat16 [8, 6312, 768], P('dp', 'head'), may hold values from -6 to 6
- frames: int32 [8], P('dp'), may hold values from 4 to 16
- text_mask: int32 [8, 40], P('dp'), may hold values 0 or 1
- latents: bfloat16 [8, 128, 768], P('dp'), may hold values from -6 to 6
- cross_q: bfloat16 [768, 768], P('head'), may hold values from -0.21875 to 0.21875
- cross_kv: bfloat16 [2, 768, 768], P(None, 'head'), may hold values from -0.21875 to 0.21875
- cross_out: bfloat16 [768, 768], P('head'), may hold values from -3.5 to 3.5
- cross_up: bfloat16 [768, 3072], P(None, 'head'), may hold values from -0.21875 to 0.21875
- cross_down: bfloat16 [3072, 768], P('head'), may hold values from -0.109375 to 0.109375
- self_qkv: bfloat16 [3, 768, 768], P(None, 'head'), may hold values from -0.21875 to 0.21875
- self_out: bfloat16 [768, 768], P('head'), may hold values from -0.875 to 0.875
- self_up: bfloat16 [768, 3072], P(None, 'head'), may hold values from -0.21875 to 0.21875
- self_down: bfloat16 [3072, 768], P('head'), may hold values from -0.109375 to 0.109375
- head_bias: float32 [2, 2, 768], P(None, None, 'head'), may hold values from -1.8 to 1.8
- up_bias: float32 [2, 3072], P(None, 'head'), may hold values from -1.8 to 1.8
- out_bias: float32 [2, 2, 768], replicated, may hold values from -1.8 to 1.8
- norm_gain: float32 [5, 768], replicated, may hold values from 0.5 to 1.5
- norm_bias: float32 [5, 768], replicated, may hold values from -1.8 to 1.8
- latents_cot: float32 [8, 128, 768], P('dp'), may hold values from -6 to 6
Outputs:
- latents_out: float32 [8, 128, 768], P('dp')
- grad_tokens: bfloat16 [8, 6312, 768], P('dp', 'head')
- grad_latents: float32 [8, 128, 768], P('dp')
- grad_cross_q: float32 [768, 768], P('head', 'dp')
- grad_cross_kv: float32 [2, 768, 768], P(None, 'head', 'dp')
- grad_cross_out: float32 [768, 768], P('head', 'dp')
- grad_cross_up: float32 [768, 3072], P('dp', 'head')
- grad_cross_down: float32 [3072, 768], P('head', 'dp')
- grad_self_qkv: float32 [3, 768, 768], P(None, 'head', 'dp')
- grad_self_out: float32 [768, 768], P('head', 'dp')
- grad_self_up: float32 [768, 3072], P('dp', 'head')
- grad_self_down: float32 [3072, 768], P('head', 'dp')
- grad_head_bias: float32 [2, 2, 768], P(None, None, 'head')
- grad_up_bias: float32 [2, 3072], P(None, 'head')
- grad_out_bias: float32 [2, 2, 768], P(None, None, 'head')
- grad_norm_gain: float32 [5, 768], P(None, 'head')
- grad_norm_bias: float32 [5, 768], P(None, 'head')
Inputs may be any that keep to these rules, and one draw needn't show every extreme that they name: The patches of frames at or after frames[c] are padding.
All inputs are finite; a program needn't handle non-finite values. No bound on the sum of `text_mask` on one device may be relied on, other than what follows from the above.
Results may differ from a plain program's by a relative error of at most 0.018.
Values may be sent and summed in bfloat16 or wider, within the bound.
A program may use at most 128 MiB of HBM per device.

v0:
```python
from functools import partial
import jax
import jax.numpy as jnp
from jax import lax
from jax.sharding import PartitionSpec as P

HD = 64
P_SIZE = 392
F_MAX = 16
EPSILON = 1e-05
NEGATIVE = -1e30


def normed(tensor, gain_row, shift_row):
    row_mean = jnp.mean(tensor, axis=-1, keepdims=True)
    centered = tensor - row_mean
    spread = jnp.mean(centered * centered, axis=-1, keepdims=True)
    return centered * lax.rsqrt(spread + EPSILON) * gain_row + shift_row


def share_of(tensor, head_index, head_width):
    return lax.dynamic_slice_in_dim(tensor, head_index * head_width, head_width, tensor.ndim - 1)


def split_heads(tensor, heads_here):
    return tensor.reshape(
        tensor.shape[0], tensor.shape[1], heads_here, tensor.shape[2] // heads_here
    )


def merge_heads(tensor):
    return tensor.reshape(tensor.shape[0], tensor.shape[1], tensor.shape[2] * tensor.shape[3])


def join_heads(partial_sum):
    return lax.psum(partial_sum.astype(jnp.bfloat16), "head").astype(jnp.float32)


def join_back(partial_sum):
    return lax.psum(partial_sum.astype(jnp.bfloat16), "head").astype(jnp.float32)


def scores_of(queries, key_rows, usable):
    scores = jnp.einsum("qhe,khe->hqk", queries, key_rows, preferred_element_type=jnp.float32)
    return jnp.where(usable[None, None, :], scores, NEGATIVE)


def attend_parts(parts):
    queries, key_rows, values, usable = parts
    scores = scores_of(queries, key_rows, usable)
    row_max = jnp.max(scores, axis=-1, keepdims=True)
    powers = jnp.exp(scores - row_max)
    totals = jnp.sum(powers, axis=-1, keepdims=True)
    chances = (powers / totals).astype(jnp.bfloat16)
    mixture = jnp.einsum("hqk,khe->qhe", chances, values, preferred_element_type=jnp.float32)
    return (mixture.astype(jnp.bfloat16), row_max, totals)


def back_parts(parts):
    queries, key_rows, values, usable, row_max, totals, grad_mix = parts
    scores = scores_of(queries, key_rows, usable)
    chances = jnp.exp(scores - row_max) / totals
    rounded = chances.astype(jnp.bfloat16)
    grad_values = jnp.einsum(
        "hqk,qhe->khe", rounded, grad_mix, preferred_element_type=jnp.float32
    ).astype(jnp.bfloat16)
    grad_chances = jnp.einsum("qhe,khe->hqk", grad_mix, values, preferred_element_type=jnp.float32)
    inner_sum = jnp.sum(chances * grad_chances, axis=-1, keepdims=True)
    grad_scores = (chances * (grad_chances - inner_sum)).astype(jnp.bfloat16)
    grad_queries = jnp.einsum(
        "hqk,khe->qhe", grad_scores, key_rows, preferred_element_type=jnp.float32
    ).astype(jnp.bfloat16)
    grad_keys = jnp.einsum(
        "hqk,qhe->khe", grad_scores, queries, preferred_element_type=jnp.float32
    ).astype(jnp.bfloat16)
    return (grad_queries, grad_keys, grad_values)


def feed_forward(tensor, gain_row, shift_row, weight_up, bias_up, weight_down):
    hidden = normed(tensor, gain_row, shift_row).astype(jnp.bfloat16)
    pre_act = (
        jnp.einsum("cnd,df->cnf", hidden, weight_up, preferred_element_type=jnp.float32) + bias_up
    )
    activation = jax.nn.gelu(pre_act, approximate=True).astype(jnp.bfloat16)
    partial_sum = jnp.einsum(
        "cnf,fd->cnd", activation, weight_down, preferred_element_type=jnp.float32
    )
    return (join_heads(partial_sum), (hidden, pre_act, activation))


def feed_back(tensor, gain_row, shift_row, weight_up, weight_down, saved_acts, grad_out):
    hidden, pre_act, activation = saved_acts
    grad_branch = grad_out.astype(jnp.bfloat16)
    grad_weight_down = jnp.einsum(
        "cnf,cnd->fd", activation, grad_branch, preferred_element_type=jnp.float32
    )
    grad_act = jnp.einsum(
        "cnd,fd->cnf", grad_branch, weight_down, preferred_element_type=jnp.float32
    )
    unused, gelu_pull = jax.vjp(partial(jax.nn.gelu, approximate=True), pre_act)
    grad_pre = gelu_pull(grad_act)[0].astype(jnp.bfloat16)
    grad_weight_up = jnp.einsum("cnd,cnf->df", hidden, grad_pre, preferred_element_type=jnp.float32)
    grad_bias_up = jnp.sum(grad_pre.astype(jnp.float32), axis=(0, 1))
    grad_hidden = join_back(
        jnp.einsum("cnf,df->cnd", grad_pre, weight_up, preferred_element_type=jnp.float32)
    )
    unused_too, norm_pull = jax.vjp(normed, tensor, gain_row, shift_row)
    grad_tensor, grad_gain, grad_shift = norm_pull(grad_hidden)
    return (grad_tensor, grad_weight_up, grad_bias_up, grad_weight_down, grad_gain, grad_shift)


def local(
    tokens,
    frames,
    text_mask,
    latents,
    cross_q,
    cross_kv,
    cross_out,
    cross_up,
    cross_down,
    self_qkv,
    self_out,
    self_up,
    self_down,
    head_bias,
    up_bias,
    out_bias,
    norm_gain,
    norm_bias,
    latents_cot,
):
    head_index = lax.axis_index("head")
    head_width = cross_q.shape[0]
    heads_here = head_width // HD
    scaling = HD ** (-0.5)
    clips_here = tokens.shape[0]
    rows_here = tokens.shape[1]
    length = rows_here * lax.axis_size("head")
    position = jnp.arange(length, dtype=jnp.int32)
    text_full = jnp.concatenate(
        [jnp.zeros((clips_here, F_MAX * P_SIZE), jnp.int32), text_mask], axis=1
    )
    usable = (position[None, :] < frames[:, None] * P_SIZE) | (text_full == 1)
    gathered, weights_whole = (
        lax.all_gather(tokens, "head", axis=1, tiled=True),
        lax.all_gather(cross_kv, "head", axis=1, tiled=True),
    )
    full_rows = gathered.astype(jnp.float32)
    row_mean = jnp.mean(full_rows, axis=-1, keepdims=True)
    centered = full_rows - row_mean
    inverse = lax.rsqrt(jnp.mean(centered * centered, axis=-1, keepdims=True) + EPSILON)
    inputs = (centered * inverse * norm_gain[0] + norm_bias[0]).astype(jnp.bfloat16)
    key_value = jnp.einsum("cld,kwd->clkw", inputs, cross_kv, preferred_element_type=jnp.float32)
    key_rows = key_value[:, :, 0].astype(jnp.bfloat16)
    cross_values = (key_value[:, :, 1] + head_bias[0, 1]).astype(jnp.bfloat16)
    start_state = latents.astype(jnp.float32)
    latent_norm = normed(start_state, norm_gain[1], norm_bias[1]).astype(jnp.bfloat16)
    cross_queries = (
        (
            jnp.einsum("cnd,wd->cnw", latent_norm, cross_q, preferred_element_type=jnp.float32)
            + head_bias[0, 0]
        )
        * scaling
    ).astype(jnp.bfloat16)
    cross_parts = (
        split_heads(cross_queries, heads_here),
        split_heads(key_rows, heads_here),
        split_heads(cross_values, heads_here),
        usable,
    )
    cross_mix, cross_max, cross_totals = lax.map(attend_parts, cross_parts)
    cross_flat = merge_heads(cross_mix)
    after_cross = (
        start_state
        + join_heads(
            jnp.einsum("cnw,wd->cnd", cross_flat, cross_out, preferred_element_type=jnp.float32)
        )
        + out_bias[0, 0]
    )
    cross_branch, cross_saved = feed_forward(
        after_cross, norm_gain[2], norm_bias[2], cross_up, up_bias[0], cross_down
    )
    after_mlp = after_cross + cross_branch + out_bias[0, 1]
    self_norm = normed(after_mlp, norm_gain[3], norm_bias[3]).astype(jnp.bfloat16)
    triple = jnp.einsum("cnd,kwd->cnkw", self_norm, self_qkv, preferred_element_type=jnp.float32)
    self_queries = ((triple[:, :, 0] + head_bias[1, 0]) * scaling).astype(jnp.bfloat16)
    self_keys = triple[:, :, 1].astype(jnp.bfloat16)
    self_values = (triple[:, :, 2] + head_bias[1, 1]).astype(jnp.bfloat16)
    everyone = jnp.ones((clips_here, self_keys.shape[1]), dtype=bool)
    self_parts = (
        split_heads(self_queries, heads_here),
        split_heads(self_keys, heads_here),
        split_heads(self_values, heads_here),
        everyone,
    )
    self_mix, self_max, self_totals = lax.map(attend_parts, self_parts)
    self_flat = merge_heads(self_mix)
    after_self = (
        after_mlp
        + join_heads(
            jnp.einsum("cnw,wd->cnd", self_flat, self_out, preferred_element_type=jnp.float32)
        )
        + out_bias[1, 0]
    )
    self_branch, self_saved = feed_forward(
        after_self, norm_gain[4], norm_bias[4], self_up, up_bias[1], self_down
    )
    latents_out = after_self + self_branch + out_bias[1, 1]
    bias_self_mlp = jnp.sum(latents_cot, axis=(0, 1))
    grad_ln_four, grad_self_up, upbias_self, grad_self_down, gain_four, shift_four = feed_back(
        after_self, norm_gain[4], norm_bias[4], self_up, self_down, self_saved, latents_cot
    )
    grad_state = latents_cot + grad_ln_four
    bias_self_attn = jnp.sum(grad_state, axis=(0, 1))
    grad_attn_in = grad_state.astype(jnp.bfloat16)
    grad_self_out = jnp.einsum(
        "cnw,cnd->wd", self_flat, grad_attn_in, preferred_element_type=jnp.float32
    )
    grad_mix = jnp.einsum(
        "cnd,wd->cnw", grad_attn_in, self_out, preferred_element_type=jnp.float32
    ).astype(jnp.bfloat16)
    self_grads = lax.map(
        back_parts, self_parts + (self_max, self_totals, split_heads(grad_mix, heads_here))
    )
    grad_query_scaled = (merge_heads(self_grads[0]).astype(jnp.float32) * scaling).astype(
        jnp.bfloat16
    )
    grad_triple = jnp.stack(
        [grad_query_scaled, merge_heads(self_grads[1]), merge_heads(self_grads[2])], axis=2
    )
    grad_self_qkv = jnp.einsum(
        "cnd,cnkw->kwd", self_norm, grad_triple, preferred_element_type=jnp.float32
    )
    bias_self_q = jnp.sum(grad_triple[:, :, 0].astype(jnp.float32), axis=(0, 1))
    bias_self_v = jnp.sum(grad_triple[:, :, 2].astype(jnp.float32), axis=(0, 1))
    grad_self_in = join_back(
        jnp.einsum("cnkw,kwd->cnd", grad_triple, self_qkv, preferred_element_type=jnp.float32)
    )
    unused, norm_pull = jax.vjp(normed, after_mlp, norm_gain[3], norm_bias[3])
    grad_ln_three, gain_three, shift_three = norm_pull(grad_self_in)
    grad_state = grad_state + grad_ln_three
    bias_cross_mlp = jnp.sum(grad_state, axis=(0, 1))
    grad_ln_two, grad_cross_up, upbias_cross, grad_cross_down, gain_two, shift_two = feed_back(
        after_cross, norm_gain[2], norm_bias[2], cross_up, cross_down, cross_saved, grad_state
    )
    grad_state = grad_state + grad_ln_two
    bias_cross_attn = jnp.sum(grad_state, axis=(0, 1))
    grad_attn_in = grad_state.astype(jnp.bfloat16)
    grad_cross_out = jnp.einsum(
        "cnw,cnd->wd", cross_flat, grad_attn_in, preferred_element_type=jnp.float32
    )
    grad_mix = jnp.einsum(
        "cnd,wd->cnw", grad_attn_in, cross_out, preferred_element_type=jnp.float32
    ).astype(jnp.bfloat16)
    cross_grads = lax.map(
        back_parts, cross_parts + (cross_max, cross_totals, split_heads(grad_mix, heads_here))
    )
    grad_query_cross = (merge_heads(cross_grads[0]).astype(jnp.float32) * scaling).astype(
        jnp.bfloat16
    )
    grad_cross_q = jnp.einsum(
        "cnd,cnw->wd", latent_norm, grad_query_cross, preferred_element_type=jnp.float32
    )
    bias_cross_q = jnp.sum(grad_query_cross.astype(jnp.float32), axis=(0, 1))
    grad_latent_in = join_back(
        jnp.einsum("cnw,wd->cnd", grad_query_cross, cross_q, preferred_element_type=jnp.float32)
    )
    unused_too, latent_pull = jax.vjp(normed, start_state, norm_gain[1], norm_bias[1])
    grad_ln_one, gain_one, shift_one = latent_pull(grad_latent_in)
    grad_latents = grad_state + grad_ln_one
    grad_pair = jnp.stack([merge_heads(cross_grads[1]), merge_heads(cross_grads[2])], axis=2)
    grad_cross_kv = jnp.einsum(
        "cld,clkw->kwd", inputs, grad_pair, preferred_element_type=jnp.float32
    )
    bias_cross_v = jnp.sum(grad_pair[:, :, 1].astype(jnp.float32), axis=(0, 1))
    arrived = lax.all_to_all(grad_pair, "head", split_axis=1, concat_axis=3, tiled=True)
    grad_share = jnp.einsum(
        "clkw,kwd->cld", arrived, weights_whole, preferred_element_type=jnp.float32
    )
    own_start = head_index * rows_here
    own_mean = lax.dynamic_slice_in_dim(row_mean, own_start, rows_here, 1)
    own_inverse = lax.dynamic_slice_in_dim(inverse, own_start, rows_here, 1)
    standard = (tokens.astype(jnp.float32) - own_mean) * own_inverse
    scaled = grad_share * norm_gain[0]
    mean_plain = jnp.mean(scaled, axis=-1, keepdims=True)
    mean_cross = jnp.mean(scaled * standard, axis=-1, keepdims=True)
    grad_tokens = (own_inverse * (scaled - mean_plain - standard * mean_cross)).astype(jnp.bfloat16)
    gain_zero, shift_zero = lax.psum(
        (jnp.sum(grad_share * standard, axis=(0, 1)), jnp.sum(grad_share, axis=(0, 1))), "head"
    )
    grad_head_bias = jnp.stack(
        [jnp.stack([bias_cross_q, bias_cross_v]), jnp.stack([bias_self_q, bias_self_v])]
    )
    grad_up_bias = jnp.stack([upbias_cross, upbias_self])
    out_full = jnp.stack(
        [jnp.stack([bias_cross_attn, bias_cross_mlp]), jnp.stack([bias_self_attn, bias_self_mlp])]
    )
    grad_out_bias = share_of(out_full, head_index, head_width)
    grad_norm_gain = share_of(
        jnp.stack([gain_zero, gain_one, gain_two, gain_three, gain_four]), head_index, head_width
    )
    grad_norm_bias = share_of(
        jnp.stack([shift_zero, shift_one, shift_two, shift_three, shift_four]),
        head_index,
        head_width,
    )
    small_sums = lax.psum(
        (grad_head_bias, grad_up_bias, grad_out_bias, grad_norm_gain, grad_norm_bias), "dp"
    )
    pieces = [
        grad_cross_q.T,
        grad_cross_kv[0].T,
        grad_cross_kv[1].T,
        grad_cross_out.T,
        grad_self_qkv[0].T,
        grad_self_qkv[1].T,
        grad_self_qkv[2].T,
        grad_self_out.T,
        grad_cross_up,
        grad_cross_down.T,
        grad_self_up,
        grad_self_down.T,
    ]
    packed = jnp.concatenate([piece.astype(jnp.bfloat16) for piece in pieces], axis=1)
    summed = lax.psum_scatter(packed, "dp", scatter_dimension=0, tiled=True).astype(jnp.float32)
    sums = []
    start = 0
    for piece in pieces:
        sums.append(summed[:, start : start + piece.shape[1]])
        start += piece.shape[1]
    return (
        latents_out,
        grad_tokens,
        grad_latents,
        sums[0].T,
        jnp.stack([sums[1].T, sums[2].T]),
        sums[3].T,
        sums[8],
        sums[9].T,
        jnp.stack([sums[4].T, sums[5].T, sums[6].T]),
        sums[7].T,
        sums[10],
        sums[11].T,
        small_sums[0],
        small_sums[1],
        small_sums[2],
        small_sums[3],
        small_sums[4],
    )


def solution(mesh):
    in_specs = (
        P("dp", "head", None),
        P("dp"),
        P("dp", None),
        P("dp", None, None),
        P("head", None),
        P(None, "head", None),
        P("head", None),
        P(None, "head"),
        P("head", None),
        P(None, "head", None),
        P("head", None),
        P(None, "head"),
        P("head", None),
        P(None, None, "head"),
        P(None, "head"),
        P(),
        P(),
        P(),
        P("dp", None, None),
    )
    out_specs = (
        P("dp", None, None),
        P("dp", "head", None),
        P("dp", None, None),
        P("head", "dp"),
        P(None, "head", "dp"),
        P("head", "dp"),
        P("dp", "head"),
        P("head", "dp"),
        P(None, "head", "dp"),
        P("head", "dp"),
        P("dp", "head"),
        P("head", "dp"),
        P(None, None, "head"),
        P(None, "head"),
        P(None, None, "head"),
        P(None, "head"),
        P(None, "head"),
    )
    return jax.shard_map(local, mesh=mesh, in_specs=in_specs, out_specs=out_specs, check_vma=False)
```

profile of v0, /device:TPU:0, one launch (start us, length us, event | category | flops | bytes accessed | tf_op | source)
XLA Modules:
  0.0 712.1 jit_solution(15768888642467319990)
XLA Ops:
  7.3 18.4 %copy.67 = bf16[1,1578,768]{2,0,1:T(2,128)(2,1)} copy(bf16[1,1578,768]{2,1,0:T(8,128)(2,1)} %param.19) | data formatting | bytes 4847616 | tf_op args[0]
  28.8 122.7 %all-gather.3.cloned.1.call-done = bf16[1,6312,768]{2,0,1:T(2,128)(2,1)} async-done(((bf16[1,1578,768]{2,0,1:T(2,128)(2,1)}), bf16[1,6312,768]{2,0,1:T(2,128)(2,1)}) %all-gather.3.cloned.1.call-update) | async-done | bytes 9695248 | tf_op jit(solution)/shard_map/all_gather | solution.py:146
  151.5 7.5 %convert_reduce_fusion = f32[6312]{0:T(1024)S(1)} fusion(bf16[1,6312,768]{2,0,1:T(2,128)(2,1)} %all-gather.3.cloned.1.call-done), kind=kLoop, calls=%fused_computation.3 | loop fusion | flops 9688920 | bytes 9720480 | tf_op jit(solution)/shard_map/reduce_sum | solution.py:150
  159.0 14.1 %fusion.4 = f32[6312]{0:T(1024)S(1)} fusion(f32[6312]{0:T(1024)S(1)} %broadcast_multiply_fusion, bf16[1,6312,768]{2,0,1:T(2,128)(2,1)} %all-gather.3.cloned.1.call-done), kind=kLoop, calls=%fused_computation.6 | loop fusion | flops 19384152 | bytes 9745728 | tf_op jit(solution)/shard_map/reduce_sum | solution.py:152
  173.2 5.6 fusion.10
  178.9 4.1 convolution_bitcast_fusion
  185.2 3.1 convolution_select_fusion
  188.3 6.2 fusion.167
  194.6 5.0 fusion.45
  201.4 31.3 %all-reduce.12.cloned.1.call-done = bf16[1,128,768]{2,1,0:T(8,128)(2,1)} async-done(((bf16[1,128,768]{2,1,0:T(8,128)(2,1)}), bf16[1,128,768]{2,1,0:T(8,128)(2,1)}) %all-reduce.12.cloned.1.call-update) | async-done | bytes 196624 | tf_op jit(solution)/shard_map/psum | solution.py:36
  239.6 30.8 %all-reduce.14.cloned.1.call-done = bf16[1,128,768]{2,1,0:T(8,128)(2,1)} async-done(((bf16[1,128,768]{2,1,0:T(8,128)(2,1)}), bf16[1,128,768]{2,1,0:T(8,128)(2,1)}) %all-reduce.14.cloned.1.call-update) | async-done | bytes 196624 | tf_op jit(solution)/shard_map/psum | solution.py:36
  280.2 32.1 %all-reduce.16.cloned.1.call-done = bf16[1,128,768]{2,1,0:T(8,128)(2,1)} async-done(((bf16[1,128,768]{2,1,0:T(8,128)(2,1)}), bf16[1,128,768]{2,1,0:T(8,128)(2,1)}) %all-reduce.16.cloned.1.call-update) | async-done | bytes 196624 | tf_op jit(solution)/shard_map/psum | solution.py:36
  316.0 2.6 convert_reduce_fusion.7
  320.7 32.1 %all-reduce.18.cloned.1.call-done = bf16[1,128,768]{2,1,0:T(8,128)(2,1)} async-done(((bf16[1,128,768]{2,1,0:T(8,128)(2,1)}), bf16[1,128,768]{2,1,0:T(8,128)(2,1)}) %all-reduce.18.cloned.1.call-update) | async-done | bytes 196624 | tf_op jit(solution)/shard_map/psum | solution.py:40
  369.1 32.1 %all-reduce.20.cloned.1.call-done = bf16[1,128,768]{2,1,0:T(8,128)(2,1)} async-done(((bf16[1,128,768]{2,1,0:T(8,128)(2,1)}), bf16[1,128,768]{2,1,0:T(8,128)(2,1)}) %all-reduce.20.cloned.1.call-update) | async-done | bytes 196624 | tf_op jit(solution)/shard_map/psum | solution.py:40
  409.8 2.4 fusion.40
  412.3 29.7 %all-reduce.22.cloned.1.call-done = bf16[1,128,768]{2,1,0:T(8,128)(2,1)} async-done(((bf16[1,128,768]{2,1,0:T(8,128)(2,1)}), bf16[1,128,768]{2,1,0:T(8,128)(2,1)}) %all-reduce.22.cloned.1.call-update) | async-done | bytes 196624 | tf_op jit(solution)/shard_map/psum | solution.py:40
  449.2 11.8 %multiply_reduce_fusion = (f32[3,128]{1,0:T(4,128)S(1)}, f32[3,128,6312]{1,2,0:T(8,128)}) fusion(f32[3,128,6312]{1,2,0:T(8,128)} %get-tuple-element.268, f32[3,128]{1,0:T(4,128)S(1)} %copy-done.87, bf16[128,3,64]{0,2,1:T(8,128)(2,1)S(1)} %bitcast.305, f32[6312,3,64]{0,2,1:T(8,128)} %bitcast.281, f32[3,64]{1,0:T(4,128)S(1)} %copy-done.98), kind=kOutput, calls=%fused_computation.16 | convolution fusion | flops 319942272 | bytes 24291072 | tf_op jit(solution)/shard_map/while/body/eval_jaxpr/qhe,khe->hqk/dot_general | solution.py:67
  461.0 9.9 %multiply_convert_fusion = bf16[3,128,6312]{1,2,0:T(8,128)(2,1)} fusion(f32[3,128,6312]{1,2,0:T(8,128)} %get-tuple-element.274, f32[3,128]{1,0:T(4,128)S(1)} %get-tuple-element.273, f32[3,128,6312]{1,2,0:T(8,128)} %get-tuple-element.268, f32[3,128]{1,0:T(4,128)S(1)} %copy-done.87), kind=kLoop, calls=%fused_computation.15 | loop fusion | flops 9695232 | bytes 24241152 | tf_op jit(solution)/shard_map/while/body/eval_jaxpr/convert_element_type | solution.py:69
  470.9 4.9 convert_reduce_fusion.11
  478.5 6.3 convert_reduce_fusion.1
  487.9 7.9 %fusion.26 = bf16[2,192,768]{2,1,0:T(8,128)(2,1)S(1)} fusion(bf16[6312,768,1]{1,0,2:T(8,128)(2,1)} %copy-done.8, bf16[1,6312,1,192]{1,3,2,0:T(8,128)(2,1)S(1)} %bitcast.282, bf16[1,6312,1,192]{1,3,2,0:T(8,128)(2,1)S(1)} %bitcast.277), kind=kOutput, calls=%fused_computation.50 | convolution fusion | flops 3725687808 | bytes 15132672 | tf_op jit(solution)/shard_map/cld,clkw->kwd/dot_general | solution.py:273
  507.9 10.3 %copy.85 = bf16[768,4608]{1,0:T(8,128)(2,1)} copy(bf16[768,4608]{0,1:T(8,128)(2,1)} %fusion.25) | data formatting | bytes 14155776
  518.2 5.6 pad_maximum_fusion
  523.8 16.4 %copy.73 = bf16[1,6312,2,192]{3,2,0,1:T(2,128)(2,1)} copy(bf16[1,6312,2,192]{1,3,2,0:T(8,128)(2,1)} %pad_maximum_fusion) | data formatting | bytes 9695232 | tf_op jit(solution)/shard_map/stack | solution.py:272
  540.4 5.5 all-to-all-start
  552.7 65.7 %all-to-all-done = bf16[1,6312,2,192]{3,2,0,1:T(2,128)(2,1)} async-done(((bf16[1,6312,2,192]{3,2,0,1:T(2,128)(2,1)}), bf16[1,6312,2,192]{3,2,0,1:T(2,128)(2,1)}, u32[]{:S(2)}, u32[]{:S(2)}) %all-to-all-start) | async-done | bytes 4847648 | tf_op jit(solution)/shard_map/all_to_all | solution.py:277
  618.4 17.0 %copy.74 = bf16[1,4,1578,2,192]{2,4,1,3,0:T(8,128)(2,1)} copy(bf16[1,4,1578,2,192]{4,3,2,1,0:T(2,128)(2,1)} %bitcast.46) | data formatting | bytes 9695232 | tf_op jit(solution)/shard_map/all_to_all | solution.py:277
  635.4 9.5 %fusion.13 = (f32[768]{0:T(1024)S(1)}, f32[1578]{0:T(1024)S(1)}, f32[1578,768,1]{1,0,2:T(8,128)S(1)}) fusion(bf16[1,1578,768]{2,1,0:T(8,128)(2,1)} %param.19, f32[1578]{0:T(1024)S(1)} %dynamic_slice.65, f32[1578]{0:T(1024)S(1)} %dynamic_slice.64, f32[768]{0:T(1024)S(1)} %copy-done.44, bf16[1578,2,768]{0,2,1:T(8,128)(2,1)} %bitcast.279, ...), kind=kOutput, calls=%fused_computation.26 | convolution fusion | flops 3732662016 | bytes 14503416 | tf_op jit(solution)/shard_map/clkw,kwd->cld/dot_general | solution.py:278
  647.8 6.2 all-reduce.2
  654.1 38.3 %all-reduce.1 = (f32[2,2,192]{2,1,0:T(2,128)}, f32[2,768]{1,0:T(2,128)}, f32[2,2,192]{2,1,0:T(2,128)}, f32[5,192]{1,0:T(8,128)}, f32[5,192]{1,0:T(8,128)}) all-reduce(f32[2,2,192]{2,1,0:T(2,128)S(1)} %pad_maximum_fusion.4, f32[2,768]{1,0:T(2,128)S(1)} %pad_maximum_fusion.3, ...), channel_id=1, replica_groups=mesh['dp'=8,'head'=4] {'dp'}, use_global_device_ids=true, to_apply=%region_39.40 | all-reduce | flops 4992 | bytes 39936 | tf_op jit(solution)/shard_map/psum | solution.py:308
  692.5 5.0 fusion.16
  (374 shorter events, 95.3 us)
Async XLA Ops:
  7.2 230.0 %copy-start = (bf16[768,768]{1,0:T(8,128)(2,1)S(1)}, bf16[768,768]{1,0:T(8,128)(2,1)}, u32[]{:S(2)}) copy-start(bf16[768,768]{1,0:T(8,128)(2,1)} %param.27) | copy-start | bytes 3538948
  7.3 144.2 %all-gather.3.cloned.1.call-start = ((), (), s32[]{:S(2)}) async-start(), calls=%async_computation.2 | async-start | bytes 24238080 | tf_op jit(solution)/shard_map/all_gather | solution.py:146
  25.7 207.0 %all-reduce.12.cloned.1.call-start = ((), (), s32[]{:S(2)}) async-start(), calls=%async_computation.3 | async-start | bytes 393216 | tf_op jit(solution)/shard_map/psum | solution.py:36
  25.9 168.6 %copy-start.97 = (f32[3,64]{1,0:T(4,128)}, f32[3,64]{1,0:T(4,128)S(1)}, u32[]{:S(2)}) copy-start(f32[3,64]{1,0:T(4,128)S(1)} %add.328) | copy-start | bytes 2308
  27.9 131.0 %copy-start.89 = (f32[768]{0:T(1024)}, f32[768]{0:T(1024)S(1)}, u32[]{:S(2)}) copy-start(f32[768]{0:T(1024)S(1)} %get-tuple-element.220) | copy-start | bytes 9220
  27.9 207.1 %copy-start.48 = (f32[768]{0:T(1024)}, f32[768]{0:T(1024)S(1)}, u32[]{:S(2)}) copy-start(f32[768]{0:T(1024)S(1)} %get-tuple-element.219) | copy-start | bytes 9220
  28.0 130.9 %copy-start.45 = (f32[768]{0:T(1024)}, f32[768]{0:T(1024)S(1)}, u32[]{:S(2)}) copy-start(f32[768]{0:T(1024)S(1)} %get-tuple-element.215) | copy-start | bytes 9220
  28.0 145.1 %copy-start.43 = (f32[768]{0:T(1024)}, f32[768]{0:T(1024)S(1)}, u32[]{:S(2)}) copy-start(f32[768]{0:T(1024)S(1)} %get-tuple-element.216) | copy-start | bytes 9220
  28.1 130.8 %copy-start.77 = (f32[128]{0:T(128)}, f32[128]{0:T(128)S(1)}, u32[]{:S(2)}) copy-start(f32[128]{0:T(128)S(1)} %broadcast_multiply_fusion.6) | copy-start | bytes 1540
  28.4 130.6 %copy-start.101 = (f32[128]{0:T(128)}, f32[128]{0:T(128)S(1)}, u32[]{:S(2)}) copy-start(f32[128]{0:T(128)S(1)} %fusion.86) | copy-start | bytes 1540
  28.4 130.6 %copy-start.94 = (f32[128]{0:T(128)}, f32[128]{0:T(128)S(1)}, u32[]{:S(2)}) copy-start(f32[128]{0:T(128)S(1)} %fusion.133) | copy-start | bytes 1540
  28.7 154.8 %copy-start.35 = (bf16[128,192]{0,1:T(8,128)(2,1)}, bf16[128,192]{0,1:T(8,128)(2,1)S(1)}, u32[]{:S(2)}) copy-start(bf16[128,192]{0,1:T(8,128)(2,1)S(1)} %fusion.44) | copy-start | bytes 147460
  199.6 70.8 %copy-start.39 = (bf16[3,64,128]{2,1,0:T(8,128)(2,1)}, bf16[3,64,128]{2,1,0:T(8,128)(2,1)S(1)}, u32[]{:S(2)}) copy-start(bf16[3,64,128]{2,1,0:T(8,128)(2,1)S(1)} %fusion.45) | copy-start | bytes 147460
  199.6 70.8 %copy-start.60 = (f32[768]{0:T(1024)S(1)}, f32[768]{0:T(1024)}, u32[]{:S(2)}) copy-start(f32[768]{0:T(1024)} %get-tuple-element.224) | copy-start | bytes 9220
  199.6 72.2 %copy-start.50 = (f32[768]{0:T(1024)S(1)}, f32[768]{0:T(1024)}, u32[]{:S(2)}) copy-start(f32[768]{0:T(1024)} %get-tuple-element.222) | copy-start | bytes 9220
  200.6 69.8 %all-reduce.14.cloned.1.call-start = ((), (), s32[]{:S(2)}) async-start(), calls=%async_computation.4 | async-start | bytes 393216 | tf_op jit(solution)/shard_map/psum | solution.py:36
  201.4 77.0 %copy-start.19 = (bf16[192,768]{1,0:T(8,128)(2,1)S(1)}, bf16[192,768]{1,0:T(8,128)(2,1)}, u32[]{:S(2)}) copy-start(bf16[192,768]{1,0:T(8,128)(2,1)} %param.29) | copy-start | bytes 884740
  237.1 77.1 %copy-start.10 = (bf16[768,768]{1,0:T(8,128)(2,1)S(1)}, bf16[768,768]{1,0:T(8,128)(2,1)}, u32[]{:S(2)}) copy-start(bf16[768,768]{1,0:T(8,128)(2,1)} %param.30) | copy-start | bytes 3538948
  238.2 74.1 %all-reduce.16.cloned.1.call-start = ((), (), s32[]{:S(2)}) async-start(), calls=%async_computation.5 | async-start | bytes 393216 | tf_op jit(solution)/shard_map/psum | solution.py:36
  280.1 72.6 %all-reduce.18.cloned.1.call-start = ((), (), s32[]{:S(2)}) async-start(), calls=%async_computation.6 | async-start | bytes 393216 | tf_op jit(solution)/shard_map/psum | solution.py:40
  320.6 82.5 %copy-start.105 = (f32[128]{0:T(128)S(1)}, f32[128]{0:T(128)}, u32[]{:S(2)}) copy-start(f32[128]{0:T(128)} %copy-done.104) | copy-start | bytes 1540
  320.6 82.5 %copy-start.53 = (f32[128]{0:T(128)S(1)}, f32[128]{0:T(128)}, u32[]{:S(2)}) copy-start(f32[128]{0:T(128)} %copy-done.52) | copy-start | bytes 1540
  320.6 82.5 %copy-start.75 = (f32[128]{0:T(128)S(1)}, f32[128]{0:T(128)}, u32[]{:S(2)}) copy-start(f32[128]{0:T(128)} %copy-done.74) | copy-start | bytes 1540
  320.6 86.1 %copy-start.15 = (f32[128,768]{1,0:T(8,128)S(1)}, f32[128,768]{1,0:T(8,128)}, u32[]{:S(2)}) copy-start(f32[128,768]{1,0:T(8,128)} %copy-done.14) | copy-start | bytes 1179652
  320.6 80.6 %all-reduce.20.cloned.1.call-start = ((), (), s32[]{:S(2)}) async-start(), calls=%async_computation.7 | async-start | bytes 393216 | tf_op jit(solution)/shard_map/psum | solution.py:40
  361.9 43.0 %copy-start.37 = (bf16[3,64,128]{2,1,0:T(8,128)(2,1)}, bf16[3,64,128]{2,1,0:T(8,128)(2,1)S(1)}, u32[]{:S(2)}) copy-start(bf16[3,64,128]{2,1,0:T(8,128)(2,1)S(1)} %get-tuple-element.277) | copy-start | bytes 147460
  369.1 72.9 %all-reduce.22.cloned.1.call-start = ((), (), s32[]{:S(2)}) async-start(), calls=%async_computation.8 | async-start | bytes 393216 | tf_op jit(solution)/shard_map/psum | solution.py:40
  407.9 41.3 %copy-start.98 = (f32[3,64]{1,0:T(4,128)S(1)}, f32[3,64]{1,0:T(4,128)}, u32[]{:S(2)}) copy-start(f32[3,64]{1,0:T(4,128)} %copy-done.97) | copy-start | bytes 2308
  409.8 138.4 %all-reduce.24.cloned.1.call-start = ((), (), s32[]{:S(2)}) async-start(), calls=%async_computation.11 | async-start | bytes 786432 | tf_op jit(solution)/shard_map/psum | solution.py:36
  476.8 158.6 %all-gather.5.cloned.1.call-start = ((), (), s32[]{:S(2)}) async-start(), calls=%async_computation.9 | async-start | bytes 2949120 | tf_op jit(solution)/shard_map/all_gather | solution.py:147
  477.5 220.0 %reduce-scatter.4.cloned.1.call-start = ((), (), s32[]{:S(2)}) async-start(), calls=%async_computation.10 | async-start | bytes 7962624
  540.4 78.0 %all-to-all-start = ((bf16[1,6312,2,192]{3,2,0,1:T(2,128)(2,1)}), bf16[1,6312,2,192]{3,2,0,1:T(2,128)(2,1)}, u32[]{:S(2)}, u32[]{:S(2)}) async-start(bf16[1,6312,2,192]{3,2,0,1:T(2,128)(2,1)} %copy.73), calls=%async_computation | async-start | bytes 12926976 | tf_op jit(solution)/shard_map/all_to_all | solution.py:277
  (89 other events, 1018.3 us)
Sparse Core Ops, SparseCore 0:
  25.9 125.5 all-gather.2
  200.7 32.0 all-reduce.11
  238.3 32.0 all-reduce.13
  280.3 32.0 all-reduce.15
  320.7 31.9 all-reduce.17
  369.2 32.0 all-reduce.19
  409.9 32.0 all-reduce.21
  476.9 32.9 all-reduce.23
  511.4 24.0 all-gather.4
  539.0 129.7 reduce-scatter.3
where the time goes:
time: 720 us; the launch traced here: 712 us
  waiting for transfers between devices  377 us (52%)
  matrix products  95.7 us (13%)
  local copies, waits for them, and re-layouts  86.2 us (12%)
  other arithmetic  85.1 us (12%)
  blocking collectives  44.6 us (6%)
  between operations  16.6 us (2%)
    all_gather x1, waiting for transfers between devices, local(): lax.all_gather(tokens, 'head', axis=1, tiled=True)  123 us
    psum x4, waiting for transfers between devices, join_heads(): lax.psum(partial_sum.astype(jnp.bfloat16), 'head').astype(jnp.float32)  94.3 us
    psum x3, waiting for transfers between devices, join_back(): lax.psum(partial_sum.astype(jnp.bfloat16), 'head').astype(jnp.float32)  93.9 us
    all_to_all x1, waiting for transfers between devices, local(): lax.all_to_all(grad_pair, 'head', split_axis=1, concat_axis=3, tiled=True)  65.7 us
    unnamed x232, local copies, waits for them, and re-layouts  45.2 us
    psum x1, blocking collectives, local(): lax.psum((grad_head_bias, grad_up_bias, grad_out_bias, grad_norm_gain, gr...  38.3 us
    all_to_all x1, local copies, waits for them, and re-layouts, local(): lax.all_to_all(grad_pair, 'head', split_axis=1, concat_axis=3, tiled=True)  17 us
    another operation x1, local copies, waits for them, and re-layouts, local(): jnp.stack([merge_heads(cross_grads[1]), merge_heads(cross_grads[2])], axi...  16.4 us
  transfers between devices with their start and end apart: 11, of which 8 were waited for; matrix products, arithmetic and copies ran while one was open for 15% of the time, Pallas kernels for 0%

commit v1 on v0

--- a/solution.py
+++ b/solution.py
@@ -9,6 +9,15 @@
 F_MAX = 16
 EPSILON = 1e-05
 NEGATIVE = -1e30
+remake_the_ladders = lambda in_array: jnp.concatenate(
+    lax.all_to_all(
+        jnp.stack(jnp.split(in_array, lax.axis_size("head"), axis=1), axis=0),
+        "head",
+        split_axis=0,
+        concat_axis=0,
+    ),
+    3,
+)
 
 
 def normed(tensor, gain_row, shift_row):
@@ -274,7 +283,7 @@
         "cld,clkw->kwd", inputs, grad_pair, preferred_element_type=jnp.float32
     )
     bias_cross_v = jnp.sum(grad_pair[:, :, 1].astype(jnp.float32), axis=(0, 1))
-    arrived = lax.all_to_all(grad_pair, "head", split_axis=1, concat_axis=3, tiled=True)
+    arrived = remake_the_ladders(grad_pair)
     grad_share = jnp.einsum(
         "clkw,kwd->cld", arrived, weights_whole, preferred_element_type=jnp.float32
     )

time: 720 us -> 692 us (0.961)
  local copies, waits for them, and re-layouts: 86.2 us -> 57.8 us
    all_to_all x1 -> x0, local copies, waits for them, and re-layouts: 17 us -> none  [local(): lax.all_to_all(grad_pair, 'head', split_axis=1, concat_axis=3, tiled=True)]
    another operation x1 -> x0, local copies, waits for them, and re-layouts: 16.4 us -> none  [local(): jnp.stack([merge_heads(cross_grads[1]), merge_heads(cross_grads[2])], axi...]
    unnamed x11, waiting for transfers between devices: 0.83 us -> 14.9 us
    all_to_all x1, waiting for transfers between devices: 65.7 us -> 52 us  [lax.all_to_all(jnp.stack(jnp.split(in_array, lax.axis_size('head'), axis=...]
    unnamed x232 -> x234, local copies, waits for them, and re-layouts: 45.2 us -> 45.3 us
  transfers between devices with their start and end apart: 11 -> 11, of which waited for: 8 -> 9; matrix products, arithmetic and copies ran while one was open for 15% -> 12% of each run, Pallas kernels for 0% -> 0%
where the time goes in v1:
time: 692 us; the launch traced here: 685 us
  waiting for transfers between devices  378 us (55%)
  matrix products  94.7 us (14%)
  other arithmetic  86.6 us (13%)
  local copies, waits for them, and re-layouts  57.8 us (8%)
  blocking collectives  44.9 us (6%)
  between operations  16.6 us (2%)
    all_gather x1, waiting for transfers between devices, local(): lax.all_gather(tokens, 'head', axis=1, tiled=True)  123 us
    psum x4, waiting for transfers between devices, join_heads(): lax.psum(partial_sum.astype(jnp.bfloat16), 'head').astype(jnp.float32)  94.3 us
    psum x3, waiting for transfers between devices, join_back(): lax.psum(partial_sum.astype(jnp.bfloat16), 'head').astype(jnp.float32)  94 us
    all_to_all x1, waiting for transfers between devices, lax.all_to_all(jnp.stack(jnp.split(in_array, lax.axis_size('head'), axis=...  52 us
    unnamed x234, local copies, waits for them, and re-layouts  45.3 us
    psum x1, blocking collectives, local(): lax.psum((grad_head_bias, grad_up_bias, grad_out_bias, grad_norm_gain, gr...  38.8 us
    unnamed x11, waiting for transfers between devices  14.9 us
    reduce_sum x1, other arithmetic, local(): jnp.mean(centered * centered, axis=-1, keepdims=True) + EPSILON  14.1 us
  transfers between devices with their start and end apart: 11, of which 9 were waited for; matrix products, arithmetic and copies ran while one was open for 12% of the time, Pallas kernels for 0%

profile of v1, /device:TPU:0, one launch (start us, length us, event | category | flops | bytes accessed | tf_op | source)
XLA Modules:
  0.0 684.8 jit_solution(6974735285664845739)
XLA Ops:
  7.3 18.4 %copy.66 = bf16[1,1578,768]{2,0,1:T(2,128)(2,1)} copy(bf16[1,1578,768]{2,1,0:T(8,128)(2,1)} %param.19) | data formatting | bytes 4847616 | tf_op args[0]
  28.8 122.7 %all-gather.3.cloned.1.call-done = bf16[1,6312,768]{2,0,1:T(2,128)(2,1)} async-done(((bf16[1,1578,768]{2,0,1:T(2,128)(2,1)}), bf16[1,6312,768]{2,0,1:T(2,128)(2,1)}) %all-gather.3.cloned.1.call-update) | async-done | bytes 9695248 | tf_op jit(solution)/shard_map/all_gather | solution.py:155
  151.5 7.5 %convert_reduce_fusion = f32[6312]{0:T(1024)S(1)} fusion(bf16[1,6312,768]{2,0,1:T(2,128)(2,1)} %all-gather.3.cloned.1.call-done), kind=kLoop, calls=%fused_computation.3 | loop fusion | flops 9688920 | bytes 9720480 | tf_op jit(solution)/shard_map/reduce_sum | solution.py:159
  159.0 14.1 %fusion.4 = f32[6312]{0:T(1024)S(1)} fusion(f32[6312]{0:T(1024)S(1)} %broadcast_multiply_fusion, bf16[1,6312,768]{2,0,1:T(2,128)(2,1)} %all-gather.3.cloned.1.call-done), kind=kLoop, calls=%fused_computation.6 | loop fusion | flops 19384152 | bytes 9745728 | tf_op jit(solution)/shard_map/reduce_sum | solution.py:161
  173.2 5.6 fusion.10
  178.9 4.1 convolution_bitcast_fusion
  185.2 3.1 convolution_select_fusion
  188.3 6.2 fusion.177
  194.6 5.0 fusion.54
  201.4 31.3 %all-reduce.12.cloned.1.call-done = bf16[1,128,768]{2,1,0:T(8,128)(2,1)} async-done(((bf16[1,128,768]{2,1,0:T(8,128)(2,1)}), bf16[1,128,768]{2,1,0:T(8,128)(2,1)}) %all-reduce.12.cloned.1.call-update) | async-done | bytes 196624 | tf_op jit(solution)/shard_map/psum | solution.py:45
  239.6 30.8 %all-reduce.14.cloned.1.call-done = bf16[1,128,768]{2,1,0:T(8,128)(2,1)} async-done(((bf16[1,128,768]{2,1,0:T(8,128)(2,1)}), bf16[1,128,768]{2,1,0:T(8,128)(2,1)}) %all-reduce.14.cloned.1.call-update) | async-done | bytes 196624 | tf_op jit(solution)/shard_map/psum | solution.py:45
  280.2 32.1 %all-reduce.16.cloned.1.call-done = bf16[1,128,768]{2,1,0:T(8,128)(2,1)} async-done(((bf16[1,128,768]{2,1,0:T(8,128)(2,1)}), bf16[1,128,768]{2,1,0:T(8,128)(2,1)}) %all-reduce.16.cloned.1.call-update) | async-done | bytes 196624 | tf_op jit(solution)/shard_map/psum | solution.py:45
  320.7 32.1 %all-reduce.18.cloned.1.call-done = bf16[1,128,768]{2,1,0:T(8,128)(2,1)} async-done(((bf16[1,128,768]{2,1,0:T(8,128)(2,1)}), bf16[1,128,768]{2,1,0:T(8,128)(2,1)}) %all-reduce.18.cloned.1.call-update) | async-done | bytes 196624 | tf_op jit(solution)/shard_map/psum | solution.py:49
  369.1 32.1 %all-reduce.20.cloned.1.call-done = bf16[1,128,768]{2,1,0:T(8,128)(2,1)} async-done(((bf16[1,128,768]{2,1,0:T(8,128)(2,1)}), bf16[1,128,768]{2,1,0:T(8,128)(2,1)}) %all-reduce.20.cloned.1.call-update) | async-done | bytes 196624 | tf_op jit(solution)/shard_map/psum | solution.py:49
  412.3 29.7 %all-reduce.22.cloned.1.call-done = bf16[1,128,768]{2,1,0:T(8,128)(2,1)} async-done(((bf16[1,128,768]{2,1,0:T(8,128)(2,1)}), bf16[1,128,768]{2,1,0:T(8,128)(2,1)}) %all-reduce.22.cloned.1.call-update) | async-done | bytes 196624 | tf_op jit(solution)/shard_map/psum | solution.py:49
  449.2 11.8 %multiply_reduce_fusion = (f32[3,128]{1,0:T(4,128)S(1)}, f32[3,128,6312]{1,2,0:T(8,128)}) fusion(f32[3,128,6312]{1,2,0:T(8,128)} %get-tuple-element.272, f32[3,128]{1,0:T(4,128)S(1)} %copy-done.87, bf16[128,3,64]{0,2,1:T(8,128)(2,1)S(1)} %bitcast.311, f32[6312,3,64]{0,2,1:T(8,128)} %bitcast.287, f32[3,64]{1,0:T(4,128)S(1)} %copy-done.98), kind=kOutput, calls=%fused_computation.16 | convolution fusion | flops 319942272 | bytes 24291072 | tf_op jit(solution)/shard_map/while/body/eval_jaxpr/qhe,khe->hqk/dot_general | solution.py:76
  461.0 9.9 %multiply_convert_fusion = bf16[3,128,6312]{1,2,0:T(8,128)(2,1)} fusion(f32[3,128,6312]{1,2,0:T(8,128)} %get-tuple-element.278, f32[3,128]{1,0:T(4,128)S(1)} %get-tuple-element.277, f32[3,128,6312]{1,2,0:T(8,128)} %get-tuple-element.272, f32[3,128]{1,0:T(4,128)S(1)} %copy-done.87), kind=kLoop, calls=%fused_computation.15 | loop fusion | flops 9695232 | bytes 24241152 | tf_op jit(solution)/shard_map/while/body/eval_jaxpr/convert_element_type | solution.py:78
  471.0 4.9 convert_reduce_fusion.11
  478.5 4.1 convolution_convert_fusion.1
  482.8 7.0 %convert_reduce_fusion.1 = (f32[3,64]{1,0:T(4,128)}, bf16[3,64,6312]{2,1,0:T(8,128)(2,1)S(1)}) fusion(bf16[128,3,64]{0,2,1:T(8,128)(2,1)S(1)} %bitcast.312, f32[3,128,6312]{1,2,0:T(8,128)} %get-tuple-element.272, f32[3,128]{1,0:T(4,128)S(1)} %copy-done.87), kind=kOutput, calls=%fused_computation.32 | convolution fusion | flops 318730560 | bytes 12170496 | tf_op jit(solution)/shard_map/while/body/eval_jaxpr/hqk,qhe->khe/dot_general | solution.py:73
  491.2 4.1 fusion.27
  507.3 10.3 %copy.83 = bf16[768,4608]{1,0:T(8,128)(2,1)} copy(bf16[768,4608]{0,1:T(8,128)(2,1)} %fusion.26) | data formatting | bytes 14155776
  517.6 4.0 fusion.31
  521.7 3.0 pad_maximum_fusion.1
  524.8 5.2 all-to-all-start
  536.9 52.0 %all-to-all-done = bf16[4,1,1578,2,192]{2,4,3,1,0:T(8,128)(2,1)} async-done(((bf16[4,1,1578,2,192]{2,4,3,1,0:T(8,128)(2,1)}), bf16[4,1,1578,2,192]{2,4,3,1,0:T(8,128)(2,1)}, u32[]{:S(2)}, u32[]{:S(2)}) %all-to-all-start) | async-done | bytes 4847648 | tf_op jit(solution)/shard_map/all_to_all | solution.py:13
  588.9 5.1 copy.72
  593.9 9.2 %fusion.14 = (f32[768]{0:T(1024)S(1)}, f32[1578]{0:T(1024)S(1)}, f32[1578,768,1]{1,0,2:T(8,128)S(1)}) fusion(bf16[1,1578,768]{2,1,0:T(8,128)(2,1)} %param.19, f32[1578]{0:T(1024)S(1)} %dynamic_slice.65, f32[1578]{0:T(1024)S(1)} %dynamic_slice.64, f32[768]{0:T(1024)S(1)} %copy-done.44, bf16[1578,2,768]{0,2,1:T(8,128)(2,1)} %bitcast.285, ...), kind=kOutput, calls=%fused_computation.35 | convolution fusion | flops 3732662016 | bytes 14503416 | tf_op jit(solution)/shard_map/clkw,kwd->cld/dot_general | solution.py:287
  606.0 6.1 all-reduce.2
  612.3 38.8 %all-reduce.1 = (f32[2,2,192]{2,1,0:T(2,128)}, f32[2,768]{1,0:T(2,128)}, f32[2,2,192]{2,1,0:T(2,128)}, f32[5,192]{1,0:T(8,128)}, f32[5,192]{1,0:T(8,128)}) all-reduce(f32[2,2,192]{2,1,0:T(2,128)S(1)} %pad_maximum_fusion.5, f32[2,768]{1,0:T(2,128)S(1)} %pad_maximum_fusion.4, ...), channel_id=1, replica_groups=mesh['dp'=8,'head'=4] {'dp'}, use_global_device_ids=true, to_apply=%region_39.40 | all-reduce | flops 4992 | bytes 39936 | tf_op jit(solution)/shard_map/psum | solution.py:317
  651.1 5.0 fusion.17
  656.1 14.1 %reduce-scatter.4.cloned.1.call-done = bf16[96,4608]{1,0:T(8,128)(2,1)} async-done(((bf16[768,4608]{1,0:T(8,128)(2,1)}), bf16[96,4608]{1,0:T(8,128)(2,1)}) %reduce-scatter.4.cloned.1.call-update) | async-done | bytes 884752
  (376 shorter events, 98.7 us)
Async XLA Ops:
  7.2 230.0 %copy-start = (bf16[768,768]{1,0:T(8,128)(2,1)S(1)}, bf16[768,768]{1,0:T(8,128)(2,1)}, u32[]{:S(2)}) copy-start(bf16[768,768]{1,0:T(8,128)(2,1)} %param.27) | copy-start | bytes 3538948
  7.3 144.2 %all-gather.3.cloned.1.call-start = ((), (), s32[]{:S(2)}) async-start(), calls=%async_computation.2 | async-start | bytes 24238080 | tf_op jit(solution)/shard_map/all_gather | solution.py:155
  25.7 207.0 %all-reduce.12.cloned.1.call-start = ((), (), s32[]{:S(2)}) async-start(), calls=%async_computation.3 | async-start | bytes 393216 | tf_op jit(solution)/shard_map/psum | solution.py:45
  25.9 168.6 %copy-start.97 = (f32[3,64]{1,0:T(4,128)}, f32[3,64]{1,0:T(4,128)S(1)}, u32[]{:S(2)}) copy-start(f32[3,64]{1,0:T(4,128)S(1)} %add.328) | copy-start | bytes 2308
  27.9 131.0 %copy-start.89 = (f32[768]{0:T(1024)}, f32[768]{0:T(1024)S(1)}, u32[]{:S(2)}) copy-start(f32[768]{0:T(1024)S(1)} %get-tuple-element.220) | copy-start | bytes 9220
  27.9 207.1 %copy-start.48 = (f32[768]{0:T(1024)}, f32[768]{0:T(1024)S(1)}, u32[]{:S(2)}) copy-start(f32[768]{0:T(1024)S(1)} %get-tuple-element.219) | copy-start | bytes 9220
  28.0 130.9 %copy-start.45 = (f32[768]{0:T(1024)}, f32[768]{0:T(1024)S(1)}, u32[]{:S(2)}) copy-start(f32[768]{0:T(1024)S(1)} %get-tuple-element.215) | copy-start | bytes 9220
  28.0 145.1 %copy-start.43 = (f32[768]{0:T(1024)}, f32[768]{0:T(1024)S(1)}, u32[]{:S(2)}) copy-start(f32[768]{0:T(1024)S(1)} %get-tuple-element.216) | copy-start | bytes 9220
  28.1 130.8 %copy-start.77 = (f32[128]{0:T(128)}, f32[128]{0:T(128)S(1)}, u32[]{:S(2)}) copy-start(f32[128]{0:T(128)S(1)} %broadcast_multiply_fusion.6) | copy-start | bytes 1540
  28.4 130.6 %copy-start.101 = (f32[128]{0:T(128)}, f32[128]{0:T(128)S(1)}, u32[]{:S(2)}) copy-start(f32[128]{0:T(128)S(1)} %fusion.95) | copy-start | bytes 1540
  28.4 130.6 %copy-start.94 = (f32[128]{0:T(128)}, f32[128]{0:T(128)S(1)}, u32[]{:S(2)}) copy-start(f32[128]{0:T(128)S(1)} %fusion.142) | copy-start | bytes 1540
  28.7 154.8 %copy-start.35 = (bf16[128,192]{0,1:T(8,128)(2,1)}, bf16[128,192]{0,1:T(8,128)(2,1)S(1)}, u32[]{:S(2)}) copy-start(bf16[128,192]{0,1:T(8,128)(2,1)S(1)} %fusion.53) | copy-start | bytes 147460
  199.6 70.8 %copy-start.39 = (bf16[3,64,128]{2,1,0:T(8,128)(2,1)}, bf16[3,64,128]{2,1,0:T(8,128)(2,1)S(1)}, u32[]{:S(2)}) copy-start(bf16[3,64,128]{2,1,0:T(8,128)(2,1)S(1)} %fusion.54) | copy-start | bytes 147460
  199.6 70.8 %copy-start.60 = (f32[768]{0:T(1024)S(1)}, f32[768]{0:T(1024)}, u32[]{:S(2)}) copy-start(f32[768]{0:T(1024)} %get-tuple-element.224) | copy-start | bytes 9220
  199.6 72.2 %copy-start.50 = (f32[768]{0:T(1024)S(1)}, f32[768]{0:T(1024)}, u32[]{:S(2)}) copy-start(f32[768]{0:T(1024)} %get-tuple-element.222) | copy-start | bytes 9220
  200.6 69.8 %all-reduce.14.cloned.1.call-start = ((), (), s32[]{:S(2)}) async-start(), calls=%async_computation.4 | async-start | bytes 393216 | tf_op jit(solution)/shard_map/psum | solution.py:45
  201.4 77.0 %copy-start.19 = (bf16[192,768]{1,0:T(8,128)(2,1)S(1)}, bf16[192,768]{1,0:T(8,128)(2,1)}, u32[]{:S(2)}) copy-start(bf16[192,768]{1,0:T(8,128)(2,1)} %param.29) | copy-start | bytes 884740
  237.1 77.1 %copy-start.10 = (bf16[768,768]{1,0:T(8,128)(2,1)S(1)}, bf16[768,768]{1,0:T(8,128)(2,1)}, u32[]{:S(2)}) copy-start(bf16[768,768]{1,0:T(8,128)(2,1)} %param.30) | copy-start | bytes 3538948
  238.2 74.1 %all-reduce.16.cloned.1.call-start = ((), (), s32[]{:S(2)}) async-start(), calls=%async_computation.5 | async-start | bytes 393216 | tf_op jit(solution)/shard_map/psum | solution.py:45
  280.1 72.6 %all-reduce.18.cloned.1.call-start = ((), (), s32[]{:S(2)}) async-start(), calls=%async_computation.6 | async-start | bytes 393216 | tf_op jit(solution)/shard_map/psum | solution.py:49
  320.6 82.5 %copy-start.105 = (f32[128]{0:T(128)S(1)}, f32[128]{0:T(128)}, u32[]{:S(2)}) copy-start(f32[128]{0:T(128)} %copy-done.104) | copy-start | bytes 1540
  320.6 82.6 %copy-start.53 = (f32[128]{0:T(128)S(1)}, f32[128]{0:T(128)}, u32[]{:S(2)}) copy-start(f32[128]{0:T(128)} %copy-done.52) | copy-start | bytes 1540
  320.6 82.6 %copy-start.75 = (f32[128]{0:T(128)S(1)}, f32[128]{0:T(128)}, u32[]{:S(2)}) copy-start(f32[128]{0:T(128)} %copy-done.74) | copy-start | bytes 1540
  320.6 86.1 %copy-start.15 = (f32[128,768]{1,0:T(8,128)S(1)}, f32[128,768]{1,0:T(8,128)}, u32[]{:S(2)}) copy-start(f32[128,768]{1,0:T(8,128)} %copy-done.14) | copy-start | bytes 1179652
  320.6 80.7 %all-reduce.20.cloned.1.call-start = ((), (), s32[]{:S(2)}) async-start(), calls=%async_computation.7 | async-start | bytes 393216 | tf_op jit(solution)/shard_map/psum | solution.py:49
  361.9 43.0 %copy-start.37 = (bf16[3,64,128]{2,1,0:T(8,128)(2,1)}, bf16[3,64,128]{2,1,0:T(8,128)(2,1)S(1)}, u32[]{:S(2)}) copy-start(bf16[3,64,128]{2,1,0:T(8,128)(2,1)S(1)} %get-tuple-element.281) | copy-start | bytes 147460
  369.1 72.9 %all-reduce.22.cloned.1.call-start = ((), (), s32[]{:S(2)}) async-start(), calls=%async_computation.8 | async-start | bytes 393216 | tf_op jit(solution)/shard_map/psum | solution.py:49
  407.9 41.3 %copy-start.98 = (f32[3,64]{1,0:T(4,128)S(1)}, f32[3,64]{1,0:T(4,128)}, u32[]{:S(2)}) copy-start(f32[3,64]{1,0:T(4,128)} %copy-done.97) | copy-start | bytes 2308
  409.8 122.5 %all-reduce.24.cloned.1.call-start = ((), (), s32[]{:S(2)}) async-start(), calls=%async_computation.11 | async-start | bytes 786432 | tf_op jit(solution)/shard_map/psum | solution.py:45
  476.8 117.1 %all-gather.5.cloned.1.call-start = ((), (), s32[]{:S(2)}) async-start(), calls=%async_computation.9 | async-start | bytes 2949120 | tf_op jit(solution)/shard_map/all_gather | solution.py:156
  477.5 192.6 %reduce-scatter.4.cloned.1.call-start = ((), (), s32[]{:S(2)}) async-start(), calls=%async_computation.10 | async-start | bytes 7962624
  524.8 64.1 %all-to-all-start = ((bf16[4,1,1578,2,192]{2,4,3,1,0:T(8,128)(2,1)}), bf16[4,1,1578,2,192]{2,4,3,1,0:T(8,128)(2,1)}, u32[]{:S(2)}, u32[]{:S(2)}) async-start(bf16[4,1,1578,2,192]{2,4,3,1,0:T(8,128)(2,1)} %pad_maximum_fusion.1), calls=%async_computation | async-start | bytes 10223616 | tf_op jit(solution)/shard_map/all_to_all | solution.py:13
  (90 other events, 1010.3 us)
Sparse Core Ops, SparseCore 0:
  25.9 125.5 all-gather.2
  200.7 32.0 all-reduce.11
  238.3 32.0 all-reduce.13
  280.3 32.0 all-reduce.15
  320.7 32.0 all-reduce.17
  369.2 32.0 all-reduce.19
  410.0 32.0 all-reduce.21
  476.9 32.9 all-reduce.23
  511.4 24.8 all-gather.4
  539.9 130.2 reduce-scatter.3
